TPU v7x, 32 devices: a whole 2x2x4 slice. The times are simulated.
32 devices in a mesh: wide: 8 (over z, y), narrow: 4 (over x, core).
Axes of the slice: x: 2, y: 2, z: 4, core: 2. Of those that a mesh axis runs over, the one named last changes fastest.
Arguments:
- rhs: float32 [3, 32, 32, 128], P(None, 'wide', 'narrow'), may hold values from -12 to 12
- start: float32 [3, 32, 32, 128], P(None, 'wide', 'narrow'), may hold values from -2 to 2
- trans: float32 [3, 32, 32, 128], P(None, 'wide', 'narrow'), may hold values from 0.2 to 2
- accum: float32 [32, 32, 128], P('wide', 'narrow'), may hold values from 2 to 8
- coupling: float32 [3, 3, 32, 32, 128], P(None, None, 'wide', 'narrow'), may hold values from -0.3 to 0.3
- well_cells: int32 [8, 4, 64], P('wide', 'narrow'), may hold values from 0 to 4095
- well_index: float32 [8, 4, 64], P('wide', 'narrow'), may hold values from 1 to 20
- agg_map: int32 [32, 32, 128], P('wide', 'narrow'), may hold values from 0 to 31
- tile_factors: bfloat16 [48, 48, 128, 128], P('wide', 'narrow')
- coarse_inverse: float32 [1024, 1024], P(('wide', 'narrow')), as said below
Outputs:
- iterate: float32 [3, 32, 32, 128], P(None, 'wide', 'narrow')
- residual: float32 [3, 32, 32, 128], P(None, 'wide', 'narrow')
Inputs may be any that keep to these rules, and one draw needn't show every extreme that they name: well_cells names, for each device's 64 connections, one of that device's own 4 * 8 * 128 cells, counted by pair, then column, then position in the tile; connections may share a cell. agg_map names one of the 32 aggregates of the device that owns the cell. coarse_inverse is symmetric.
All inputs are finite; a program needn't handle non-finite values.
Results may differ from a plain program's by a relative error of at most 0.00095.
Values sent between devices are 32-bit elements; how exact they have to be, the bound alone decides.
A program may use at most 64 MiB of HBM per device.

v0:
```python
import functools

import jax
import jax.numpy as jnp
from jax import lax
from jax.experimental import pallas as pl
from jax.experimental.pallas import tpu as pltpu
from jax.sharding import PartitionSpec as P

SWEEPS = 3
HIGHEST = lax.Precision.HIGHEST
NT = (((1,), (1,)), ((), ()))
F32 = jnp.float32

DIRS = ((-1, 0), (1, 0), (0, -1), (0, 1), (-1, -1), (-1, 1), (1, -1), (1, 1))


def halo_piece(d, px, cy, depth_x, depth_y):
    dx, dy = d
    if dx == 0:
        sp, dp, npair = 2, 2, px
    elif dx > 0:
        sp, dp, npair = 2 + px - depth_x, 2 - depth_x, depth_x
    else:
        sp, dp, npair = 2, 2 + px, depth_x
    if dy == 0:
        sr, dr, nrow = 0, 0, cy
    elif dy > 0:
        sr, dr, nrow = cy - depth_y, 2 * cy - depth_y, depth_y
    else:
        sr, dr, nrow = 0, cy, depth_y
    return (pl.ds(sp, npair), pl.ds(sr, nrow)), (pl.ds(dp, npair), pl.ds(dr, nrow))


def body(
    nw, nn,
    rhs, start, trans, accum, coupling, cells, widx, agg, tiles, cinv,
    out_it, out_res,
    COEF, CUR, FIX, W1, W2, H, DER, TF, CI, AG, AGX, ACC, GB, YB,
    loc, hs, hr, cs, cr, gs, gr, is_, ir,
):
    phases = rhs.shape[0]
    px, cy, tile = accum.shape
    box = px + 2
    half = tile // 2
    aggs = CI.shape[0]
    me_w, me_n = lax.axis_index("wide"), lax.axis_index("narrow")

    def dev(dw, dn):
        return {"wide": lax.rem(me_w + dw + nw, nw), "narrow": lax.rem(me_n + dn + nn, nn)}

    own = pl.ds(2, px)
    top = pl.ds(0, cy)
    nch = COEF.shape[0]
    first_rhs = nch - phases
    copies = [
        (accum, ACC),
        (trans, COEF.at[pl.ds(0, 3), own, top]),
        (start, CUR.at[0, :, own, top]),
        (coupling, COEF.at[pl.ds(4, phases * phases), own, top]),
        (rhs, COEF.at[pl.ds(first_rhs, phases), own, top]),
        (agg, AG),
        (cinv, CI),
        (tiles, TF),
    ]
    local = [pltpu.make_async_copy(s, d, loc.at[k]) for k, (s, d) in enumerate(copies)]
    for c in local:
        c.start()

    barrier = pltpu.get_barrier_semaphore()
    peers = [(dw, dn) for dw in range(nw) for dn in range(nn) if dw or dn]
    for p in range(px + 4):
        AGX[p] = jnp.zeros((2 * cy, tile), jnp.int32)
    for d in peers:
        pl.semaphore_signal(barrier, inc=1, device_id=dev(*d), device_id_type=pl.DeviceIdType.MESH)

    conn = cells.shape[-1]
    cell_row = cells[...]
    rows_own = px * cy
    hit_r = lax.broadcasted_iota(jnp.int32, (rows_own, conn), 0) == cell_row // tile
    hit_l = lax.broadcasted_iota(jnp.int32, (tile, conn), 0) == cell_row % tile
    left = jnp.where(hit_r, jnp.broadcast_to(widx[...], (rows_own, conn)), 0.0)
    right = jnp.where(hit_l, 1.0, 0.0)
    wells = lax.dot_general(left, right, NT, precision=HIGHEST, preferred_element_type=F32)
    local[0].wait()
    COEF[3, 2 : 2 + px, 0:cy, :] = ACC[...] + wells.reshape(px, cy, tile)
    for c in local[1:5]:
        c.wait()
    pl.semaphore_wait(barrier, len(peers))

    def remote(src, dst, ss, rs, d):
        return pltpu.make_async_remote_copy(
            src_ref=src, dst_ref=dst, send_sem=ss, recv_sem=rs,
            device_id=dev(*d), device_id_type=pl.DeviceIdType.MESH,
        )

    def halo(e):
        out = []
        for k, d in enumerate(DIRS):
            src, dst = halo_piece(d, px, cy, 2, 2 if d[0] else 3)
            out.append(remote(CUR.at[(e, slice(None)) + src], CUR.at[(e, slice(None)) + dst],
                              hs.at[e, k], hr.at[e, k], d))
        return out

    coef = []

    def send_coef(channels, src, dst, d):
        k = len(coef)
        coef.append(remote(COEF.at[(channels,) + src], COEF.at[(channels,) + dst], cs.at[k], cr.at[k], d))

    for d in DIRS:
        depth_y = 1 if d[0] < 0 else 2
        src, dst = halo_piece(d, px, cy, 1, depth_y)
        send_coef(pl.ds(0, nch), src, dst, d)
        if d[0] > 0:
            (_, sr), (_, dr) = src, dst
            send_coef(pl.ds(0, 1), (pl.ds(px, 1), sr), (pl.ds(0, 1), dr), d)
        if d[1] > 0:
            (sp, _), (dp, _) = src, dst
            send_coef(pl.ds(1, 1), (sp, pl.ds(cy - depth_y - 1, 1)), (dp, pl.ds(2 * cy - depth_y - 1, 1)), d)

    aggregates = []
    for k, d in enumerate(DIRS):
        src, dst = halo_piece(d, px, cy, 2, 2 if d[0] else 3)
        aggregates.append(remote(AGX.at[src], AGX.at[dst], is_.at[k], ir.at[k], d))
    for c in halo(0) + coef:
        c.start()
    local[5].wait()
    AGX[2 : 2 + px, 0:cy] = (AG[...] + me_n * aggs).reshape(px, cy, tile)
    for c in aggregates:
        c.start()

    lane = lax.broadcasted_iota(jnp.int32, (2 * cy, tile), 1)
    low = lane < half
    roll = pltpu.roll

    zero16 = jnp.zeros((2 * cy, tile), F32)
    for c in range(phases):
        for w in (W1, W2):
            w[c, 0] = zero16
            w[c, box + 1] = zero16
        W2[c, 1] = zero16
        W2[c, box] = zero16
    for c in local[6:]:
        c.wait()
    for c in coef:
        c.wait_recv()

    for b in range(box):
        tx = COEF[0, b + 1]
        txw = jnp.where(low, roll(COEF[0, b], half, 1), roll(tx, half, 1))
        ty = COEF[1, b + 1]
        tys = roll(ty, 1, 0)
        tz = jnp.where(lane % half < half - 1, COEF[2, b + 1], 0.0)
        tzd = roll(tz, 1, 1)
        centre = COEF[3, b + 1] + (tx + txw + ty + tys + tz + tzd)
        DER[0, b] = txw
        DER[1, b] = tys
        DER[2, b] = tz
        DER[3, b] = tzd
        for c in range(phases):
            diag = centre + COEF[4 + c * phases + c, b + 1]
            DER[4 + c, b] = diag
            DER[4 + phases + c, b] = 1.0 / diag

    def operate(read, boxes):
        swapped = {}

        def swap(c, idx):
            if (c, idx) not in swapped:
                swapped[c, idx] = roll(read(c, idx), half, 1)
            return swapped[c, idx]

        for b in boxes:
            values = [read(c, b + 1) for c in range(phases)]
            result = []
            for c in range(phases):
                v = values[c]
                east = jnp.where(low, swap(c, b + 1), swap(c, b + 2))
                west = jnp.where(low, swap(c, b), swap(c, b + 1))
                total = DER[4 + c, b] * v
                for o in range(phases):
                    if o != c:
                        total = total + COEF[4 + c * phases + o, b + 1] * values[o]
                inflow = COEF[0, b + 1] * east + DER[0, b] * west
                inflow = inflow + COEF[1, b + 1] * roll(v, 2 * cy - 1, 0)
                inflow = inflow + DER[1, b] * roll(v, 1, 0)
                inflow = inflow + DER[2, b] * roll(v, tile - 1, 1)
                inflow = inflow + DER[3, b] * roll(v, 1, 1)
                result.append(total - inflow)
            yield b, result

    row = lax.broadcasted_iota(jnp.int32, (phases * cy, tile), 0) % cy

    def product(b, q, chosen):
        stack = jnp.concatenate(q, axis=0)
        lhs = jnp.concatenate(
            [jnp.where(row == r, stack, 0.0) for r, _ in chosen], axis=1).astype(jnp.bfloat16)
        factors = jnp.concatenate([TF[b, t] for _, t in chosen], axis=1)
        out = lax.dot_general(lhs, factors, NT, preferred_element_type=F32)
        return [out[c * cy : (c + 1) * cy] for c in range(phases)]

    ring_a = tuple((y, y + 2) for y in range(cy))
    ring_b = ((0, cy + 2), (1, cy + 3), (cy - 2, 0), (cy - 1, 1))
    near_b = ((0, cy + 2), (cy - 1, 1))
    inner = range(1, box - 1)

    def scaled(b, h):
        return [DER[4 + phases + c, b] * h[c] for c in range(phases)]

    agg_iota = lax.broadcasted_iota(jnp.int32, (aggs, tile), 0)

    def current(e):
        return lambda c, idx: FIX[idx] if c == 0 else CUR[e, c, idx]

    def sweep(s, carry):
        read = current(s)
        acc = jnp.zeros((aggs, tile), F32)
        for b, applied in operate(read, inner):
            h = [COEF[first_rhs + c, b + 1] - applied[c] for c in range(phases)]
            for c in range(phases):
                H[c, b] = h[c]
            if True:
                for y in range(cy):
                    ids = AG[pl.ds((b - 1) * cy + y, 1), :]
                    acc = acc + jnp.where(agg_iota == ids, h[0][y : y + 1], 0.0)
        sums = jnp.broadcast_to(jnp.sum(acc, axis=1, keepdims=True), (aggs, tile))
        for g in range(nw):
            y = jnp.sum(CI[:, g * tile : (g + 1) * tile] * sums, axis=0, keepdims=True)
            for k in range(3):
                YB[s, (g + 1 - k) % nw, k : k + 1] = y
        share = [remote(YB.at[s, lax.rem(me_w + d[0], nw)], GB.at[s, k], gs.at[k], gr.at[s, k], d)
                 for k, d in enumerate(peers)]
        for c in share:
            c.start()
        for b, applied in operate(read, (0, box - 1)):
            for c in range(phases):
                H[c, b] = COEF[first_rhs + c, b + 1] - applied[c]

        for b in range(box):
            q = scaled(b, [H[c, b] for c in range(phases)])
            upper = product(b, [v[:cy] for v in q], ring_a)
            lower = product(b, [v[cy:] for v in q], ring_b if b in inner else near_b)
            for c in range(phases):
                W1[c, b + 1, 0:cy] = upper[c]
                W1[c, b + 1, cy : 2 * cy] = lower[c]

        for b, applied in operate(lambda c, idx: W1[c, idx], range(box)):
            q = scaled(b, [H[c, b] - applied[c] for c in range(phases)])
            upper = product(b, [v[:cy] for v in q], ring_a)
            for c in range(phases):
                W2[c, b + 1, 0:cy] = W1[c, b + 1, 0:cy] + upper[c]
            if b in inner:
                lower = product(b, [v[cy:] for v in q], near_b)
                for c in range(phases):
                    W2[c, b + 1, cy : 2 * cy] = W1[c, b + 1, cy : 2 * cy] + lower[c]

        for b, applied in operate(lambda c, idx: W2[c, idx], inner):
            q = scaled(b, [H[c, b] - applied[c] for c in range(phases)])
            upper = product(b, [v[:cy] for v in q], ring_a)
            for c in range(phases):
                W1[c, b + 1, 0:cy] = W2[c, b + 1, 0:cy] + upper[c]

        for c in range(phases):
            for p in range(px):
                CUR[s + 1, c, p + 2, 0:cy] = read(c, p + 2)[:cy] + W1[c, p + 2, 0:cy]
        for c in halo(s + 1):
            c.start()
        for c in share:
            c.wait_recv()
        total = YB[s, me_w]
        for k in range(len(peers)):
            total = total + GB[s, k]
        tables = [jnp.broadcast_to(total[k : k + 1], (2 * cy, tile)) for k in range(3)]
        for c in halo(s + 1):
            c.wait_recv()
        for p in range(px + 4):
            table = tables[0 if p < 2 else 1 if p < 2 + px else 2]
            lifted = jnp.take_along_axis(table, AGX[p], axis=1, mode="promise_in_bounds")
            FIX[p] = CUR[s + 1, 0, p] + lifted
        for c in share + halo(s):
            c.wait_send()
        return carry

    for c in halo(0):
        c.wait_recv()
    for p in range(px + 4):
        FIX[p] = CUR[0, 0, p]
    for c in aggregates:
        c.wait_recv()
    lax.fori_loop(0, SWEEPS, sweep, 0)
    last = current(SWEEPS)
    for c in range(phases):
        for p in range(px):
            out_it[c, p] = last(c, p + 2)[:cy]
    for b, applied in operate(last, inner):
        for c in range(phases):
            out_res[c, b - 1] = COEF[first_rhs + c, b + 1, 0:cy] - applied[c][:cy]
    for c in halo(SWEEPS) + coef + aggregates:
        c.wait_send()


def hand_over(iterate, residual, out_it, out_res):
    out_it[...] = iterate[...]
    out_res[...] = residual[...]


def solution(mesh):
    nw, nn = mesh.shape["wide"], mesh.shape["narrow"]

    def per_device(rhs, start, trans, accum, coupling, well_cells, well_index, agg_map, tile_factors, coarse_inverse):
        phases, px, cy, tile = rhs.shape
        box = px + 2
        aggs = coarse_inverse.shape[0]
        nch = 4 + phases * phases + phases
        vmem = pl.BlockSpec(memory_space=pltpu.VMEM)
        hbm = pl.BlockSpec(memory_space=pl.ANY)
        shape = jax.ShapeDtypeStruct(rhs.shape, F32)
        ring = (2 * cy, tile)
        dma = pltpu.SemaphoreType.DMA
        call = pl.pallas_call(
            functools.partial(body, nw, nn),
            out_shape=(shape, shape),
            in_specs=[hbm, hbm, hbm, hbm, hbm, vmem, vmem, hbm, hbm, hbm],
            out_specs=(vmem, vmem),
            scratch_shapes=[
                pltpu.VMEM((nch, px + 4) + ring, F32),
                pltpu.VMEM((SWEEPS + 1, phases, px + 4) + ring, F32),
                pltpu.VMEM((px + 4,) + ring, F32),
                pltpu.VMEM((phases, px + 4) + ring, F32),
                pltpu.VMEM((phases, px + 4) + ring, F32),
                pltpu.VMEM((phases, box) + ring, F32),
                pltpu.VMEM((4 + 2 * phases, box) + ring, F32),
                pltpu.VMEM(tile_factors.shape, tile_factors.dtype),
                pltpu.VMEM(coarse_inverse.shape, F32),
                pltpu.VMEM((px * cy, tile), jnp.int32),
                pltpu.VMEM((px + 4,) + ring, jnp.int32),
                pltpu.VMEM(accum.shape, F32),
                pltpu.VMEM((SWEEPS, nw * nn - 1, 3, tile), F32),
                pltpu.VMEM((SWEEPS, nw, 3, tile), F32),
                dma((8,)),
                dma((SWEEPS + 1, len(DIRS))),
                dma((SWEEPS + 1, len(DIRS))),
                dma((14,)),
                dma((14,)),
                dma((nw * nn - 1,)),
                dma((SWEEPS, nw * nn - 1)),
                dma((len(DIRS),)),
                dma((len(DIRS),)),
            ],
            compiler_params=pltpu.CompilerParams(collective_id=0, has_side_effects=True),
            name="schwarz",
        )
        held = call(
            rhs, start, trans, accum,
            coupling.reshape((phases * phases,) + accum.shape),
            well_cells.reshape(1, -1), well_index.reshape(1, -1),
            agg_map.reshape(px * cy, tile), tile_factors, coarse_inverse)
        return pl.pallas_call(
            hand_over, out_shape=(shape, shape), in_specs=[vmem, vmem], out_specs=(vmem, vmem),
            name="hand_over",
        )(*held)

    return jax.shard_map(
        per_device,
        mesh=mesh,
        in_specs=(
            P(None, "wide", "narrow", None),
            P(None, "wide", "narrow", None),
            P(None, "wide", "narrow", None),
            P("wide", "narrow", None),
            P(None, None, "wide", "narrow", None),
            P("wide", "narrow", None),
            P("wide", "narrow", None),
            P("wide", "narrow", None),
            P("wide", "narrow", None, None),
            P(("wide", "narrow"), None),
        ),
        out_specs=(P(None, "wide", "narrow", None), P(None, "wide", "narrow", None)),
        check_vma=False,
    )
```

profile of v0, /device:TPU:0, one launch (start us, length us, event | category | flops | bytes accessed | tf_op | source)
XLA Modules:
  0.0 40.1 jit_solution(14894893400179467076)
XLA Ops:
  0.6 38.0 %schwarz.1 = (f32[3,4,8,128]{3,2,1,0:T(8,128)}, f32[3,4,8,128]{3,2,1,0:T(8,128)}) custom-call(f32[3,4,8,128]{3,2,1,0:T(8,128)} %rhs.1, f32[3,4,8,128]{3,2,1,0:T(8,128)} %start.1, f32[3,4,8,128]{3,2,1,0:T(8,128)} %trans.1, f32[4,8,128]{2,1,0:T(8,128)} %accum.1, f32[9,4,8,128]{3,2,1,0:T(8,128)} %bitcast.4, s32[1,64]{1,0:T(1,128)} %bitcast.6, f32[1,64]{1,0:T(1,128)} %bitcast.7, ...), custom_call_target="tpu_custom_call" | custom-call | tf_op jit(solution)/shard_map/schwarz/pallas_call | solution.py:354
  38.7 1.5 %hand_over.1 = (f32[3,4,8,128]{3,2,1,0:T(8,128)}, f32[3,4,8,128]{3,2,1,0:T(8,128)}) custom-call(f32[3,4,8,128]{3,2,1,0:T(8,128)} %get-tuple-element.4.iterate, f32[3,4,8,128]{3,2,1,0:T(8,128)} %get-tuple-element.5.residual), custom_call_target="tpu_custom_call" | custom-call | tf_op jit(solution)/shard_map/hand_over/pallas_call | solution.py:359
where the time goes:
time: 40.4 us; the launch traced here: 40.1 us
  Pallas kernels  39.5 us (98%)
  between operations  0.64 us (2%)
    pallas_call x1, Pallas kernels, per_device(): call(rhs, start, trans, accum, coupling.reshape((phases * phases,) + accu...  38 us
    pallas_call x1, Pallas kernels, per_device(): pl.pallas_call(hand_over, out_shape=(shape, shape), in_specs=[vmem, vmem]...  1.46 us

commit v1 on v0

v1 whole, which is shorter than its diff:
```python
import functools

import jax
import jax.numpy as jnp
from jax import lax
from jax.experimental import pallas as pl
from jax.experimental.pallas import tpu as pltpu
from jax.sharding import PartitionSpec as P

SWEEPS = 3
HIGHEST = lax.Precision.HIGHEST
NT = (((1,), (1,)), ((), ()))
F32 = jnp.float32

DIRS = ((-1, 0), (1, 0), (0, -1), (0, 1), (-1, -1), (-1, 1), (1, -1), (1, 1))
UP_FIRST = (1, 6, 7, 2, 3, 0, 4, 5)
DOWN_FIRST = (0, 4, 5, 2, 3, 1, 6, 7)
ACW, TX, TY, TZ = range(4)


def slot(t, cy):
    if t < cy:
        return t + 2
    return t + 2 if t < cy + 2 else t - cy - 2


def halo_piece(d, px, cy, depth_x, depth_y):
    dx, dy = d
    if dx == 0:
        sp, dp, npair = 2, 2, px
    elif dx > 0:
        sp, dp, npair = 2 + px - depth_x, 2 - depth_x, depth_x
    else:
        sp, dp, npair = 2, 2 + px, depth_x
    if dy == 0:
        sr, dr, nrow = 0, 0, cy
    elif dy > 0:
        sr, dr, nrow = cy - depth_y, 2 * cy - depth_y, depth_y
    else:
        sr, dr, nrow = 0, cy, depth_y
    return (pl.ds(sp, npair), pl.ds(sr, nrow)), (pl.ds(dp, npair), pl.ds(dr, nrow))


def body(
    nw, nn,
    rhs, start, trans, accum, coupling, cells, widx, agg, tiles, cinv,
    out_it, out_res,
    COEF, CUR, FIX, W1, W2, H, DER, TF, WT, CI, AG, AGX, ACC, CELLS, WIDX, GB, YB,
    loc, hs, hr, cs, cr, gs, gr, is_, ir, near, far,
):
    phases = rhs.shape[0]
    px, cy, tile = accum.shape
    box = px + 2
    half = tile // 2
    aggs = CI.shape[0]
    me_w, me_n = lax.axis_index("wide"), lax.axis_index("narrow")

    def dev(dw, dn):
        return {"wide": lax.rem(me_w + dw + nw, nw), "narrow": lax.rem(me_n + dn + nn, nn)}

    own = pl.ds(2, px)
    top = pl.ds(0, cy)
    nch = COEF.shape[0]
    first_rhs = nch - phases
    copies = [
        (cells, CELLS),
        (widx, WIDX),
        (accum, ACC),
        (trans, COEF.at[pl.ds(1, 3), own, top]),
        (start, CUR.at[0, :, own, top]),
        (coupling, COEF.at[pl.ds(4, phases * phases), own, top]),
        (rhs, COEF.at[pl.ds(first_rhs, phases), own, top]),
        (agg, AG),
        (cinv, CI),
        (tiles, TF),
    ]
    local = [pltpu.make_async_copy(s, d, loc.at[k]) for k, (s, d) in enumerate(copies)]
    for c in local:
        c.start()

    peers = [(dw, dn) for dw in range(nw) for dn in range(nn) if dw or dn]

    def signal(sem, d):
        pl.semaphore_signal(sem, inc=1, device_id=dev(*d), device_id_type=pl.DeviceIdType.MESH)

    barrier = pltpu.get_barrier_semaphore()
    for p in range(px + 4):
        AGX[p] = jnp.zeros((2 * cy, tile), jnp.int32)
    for d in DIRS:
        signal(barrier, d)

    def remote(src, dst, ss, rs, d):
        return pltpu.make_async_remote_copy(
            src_ref=src, dst_ref=dst, send_sem=ss, recv_sem=rs,
            device_id=dev(*d), device_id_type=pl.DeviceIdType.MESH,
        )

    def halo(e):
        out = []
        for k, d in enumerate(DIRS):
            src, dst = halo_piece(d, px, cy, 2, 2 if d[0] else 3)
            out.append(remote(CUR.at[(e, slice(None)) + src], CUR.at[(e, slice(None)) + dst],
                              hs.at[e, k], hr.at[e, k], d))
        return out

    coef, bulk, late = [], ([], []), ([], [])

    def send_coef(channels, src, dst, d):
        k = len(coef)
        coef.append(remote(COEF.at[(channels,) + src], COEF.at[(channels,) + dst], cs.at[k], cr.at[k], d))
        return coef[-1]

    pieces = []
    for d in DIRS:
        depth_y = 1 if d[0] < 0 else 2
        src, dst = halo_piece(d, px, cy, 1, depth_y)
        main = [send_coef(pl.ds(1, nch - 1), src, dst, d)]
        rest = [send_coef(pl.ds(ACW, 1), src, dst, d)]
        if d[0] > 0:
            (_, sr), (_, dr) = src, dst
            rest.append(send_coef(pl.ds(1, 1), (pl.ds(px, 1), sr), (pl.ds(0, 1), dr), d))
        if d[1] > 0:
            (sp, _), (dp, _) = src, dst
            rest.append(send_coef(pl.ds(2, 1), (sp, pl.ds(cy - depth_y - 1, 1)), (dp, pl.ds(2 * cy - depth_y - 1, 1)), d))
        pieces.append((main, rest))
    for k in UP_FIRST:
        bulk[0].extend(pieces[k][0])
        late[0].extend(pieces[k][1])
    for k in DOWN_FIRST:
        bulk[1].extend(pieces[k][0])
        late[1].extend(pieces[k][1])

    aggregates = []
    for k, d in enumerate(DIRS):
        src, dst = halo_piece(d, px, cy, 2, 2 if d[0] else 3)
        aggregates.append(remote(AGX.at[src], AGX.at[dst], is_.at[k], ir.at[k], d))
    odd = lax.rem(me_w, 2)

    def start_all(first, second):
        @pl.when(odd == 1)
        def _():
            for c in first:
                c.start()

        @pl.when(odd == 0)
        def _():
            for c in second:
                c.start()

    local[4].wait()
    pl.semaphore_wait(barrier, len(DIRS))
    for d in DIRS:
        signal(near, d)
    begin = halo(0)
    start_all([begin[k] for k in UP_FIRST], [begin[k] for k in DOWN_FIRST])
    for c in (local[3], local[5], local[6]):
        c.wait()
    start_all(*bulk)
    conn = cells.shape[-1]
    for c in local[:3]:
        c.wait()
    cell_row = CELLS[...]
    rows_own = px * cy
    hit_r = lax.broadcasted_iota(jnp.int32, (rows_own, conn), 0) == cell_row // tile
    hit_l = lax.broadcasted_iota(jnp.int32, (tile, conn), 0) == cell_row % tile
    left = jnp.where(hit_r, jnp.broadcast_to(WIDX[...], (rows_own, conn)), 0.0)
    right = jnp.where(hit_l, 1.0, 0.0)
    wells = lax.dot_general(left, right, NT, precision=HIGHEST, preferred_element_type=F32)
    COEF[ACW, 2 : 2 + px, 0:cy, :] = ACC[...] + wells.reshape(px, cy, tile)
    start_all(*late)
    local[7].wait()
    AGX[2 : 2 + px, 0:cy] = (AG[...] + me_n * aggs).reshape(px, cy, tile)
    for c in aggregates:
        c.start()

    lane = lax.broadcasted_iota(jnp.int32, (2 * cy, tile), 1)
    low = lane < half
    roll = pltpu.roll

    zero16 = jnp.zeros((2 * cy, tile), F32)
    for c in range(phases):
        for w in (W1, W2):
            w[c, 0] = zero16
            w[c, box + 1] = zero16
        W2[c, 1] = zero16
        W2[c, box] = zero16
    local[9].wait()
    half_y = cy // 2
    for b in range(box):
        for t in range(cy + 4):
            if t < cy:
                kb, nb = t % half_y, t // half_y
            else:
                kb, nb = half_y + (t - cy) % 2, (t - cy) // 2
            WT[b, kb * tile : (kb + 1) * tile, nb * tile : (nb + 1) * tile] = TF[b, slot(t, cy)].T
    pl.semaphore_wait(near, len(DIRS))
    reach, k = 2, 0
    while reach < max(nw // 2, nn // 2):
        ws = (0,) if reach >= nw // 2 else (-reach, 0, reach)
        ns = (0,) if reach >= nn // 2 else (-reach, 0, reach)
        ring_of = [(a, c) for a in ws for c in ns if a or c]
        for d in ring_of:
            signal(far.at[k], d)
        pl.semaphore_wait(far.at[k], len(ring_of))
        reach, k = 2 * reach, k + 1
    local[8].wait()
    for c in coef:
        c.wait_recv()

    for b in range(box):
        tx = COEF[TX, b + 1]
        txw = jnp.where(low, roll(COEF[TX, b], half, 1), roll(tx, half, 1))
        ty = COEF[TY, b + 1]
        tys = roll(ty, 1, 0)
        tz = jnp.where(lane % half < half - 1, COEF[TZ, b + 1], 0.0)
        tzd = roll(tz, 1, 1)
        centre = COEF[ACW, b + 1] + (tx + txw + ty + tys + tz + tzd)
        DER[0, b] = txw
        DER[1, b] = tys
        DER[2, b] = tz
        DER[3, b] = tzd
        for c in range(phases):
            diag = centre + COEF[4 + c * phases + c, b + 1]
            DER[4 + c, b] = diag
            DER[4 + phases + c, b] = 1.0 / diag

    def operate(read, boxes):
        swapped = {}

        def swap(c, idx):
            if (c, idx) not in swapped:
                swapped[c, idx] = roll(read(c, idx), half, 1)
            return swapped[c, idx]

        for b in boxes:
            values = [read(c, b + 1) for c in range(phases)]
            result = []
            for c in range(phases):
                v = values[c]
                east = jnp.where(low, swap(c, b + 1), swap(c, b + 2))
                west = jnp.where(low, swap(c, b), swap(c, b + 1))
                total = DER[4 + c, b] * v
                for o in range(phases):
                    if o != c:
                        total = total + COEF[4 + c * phases + o, b + 1] * values[o]
                inflow = COEF[TX, b + 1] * east + DER[0, b] * west
                inflow = inflow + COEF[TY, b + 1] * roll(v, 2 * cy - 1, 0)
                inflow = inflow + DER[1, b] * roll(v, 1, 0)
                inflow = inflow + DER[2, b] * roll(v, tile - 1, 1)
                inflow = inflow + DER[3, b] * roll(v, 1, 1)
                result.append(total - inflow)
            yield b, result

    row = lax.broadcasted_iota(jnp.int32, (2 * cy, tile), 0)
    upper_half = ((row >= half_y) & (row < cy)) | (row >= 2 * cy - 2)
    own_blocks = [(row < cy) & (row % half_y == j) for j in range(half_y)]
    near_rows = (row == cy, row == 2 * cy - 1)
    ring_rows = ((row == cy) | (row == 2 * cy - 2), (row == cy + 1) | (row == 2 * cy - 1))

    def product(b, q, extra):
        n = cy if extra is None else 2 * cy
        blocks = own_blocks + list(extra or ())
        stack = jnp.concatenate([v[:n] for v in q], axis=0)
        masks = [jnp.concatenate([m[:n]] * phases, axis=0) for m in blocks]
        lhs = jnp.concatenate([jnp.where(m, stack, 0.0) for m in masks], axis=1).astype(jnp.bfloat16)
        out = jnp.dot(lhs, WT[b, : len(blocks) * tile, :], preferred_element_type=F32)
        return [jnp.where(upper_half[:n], out[c * n : (c + 1) * n, tile:], out[c * n : (c + 1) * n, :tile])
                for c in range(phases)]

    inner = range(1, box - 1)

    def scaled(b, h):
        return [DER[4 + phases + c, b] * h[c] for c in range(phases)]

    agg_iota = lax.broadcasted_iota(jnp.int32, (aggs, tile), 0)

    def current(e):
        return lambda c, idx: FIX[idx] if c == 0 else CUR[e, c, idx]

    def sweep(s, carry):
        read = current(s)
        acc = jnp.zeros((aggs, tile), F32)
        for b, applied in operate(read, inner):
            h = [COEF[first_rhs + c, b + 1] - applied[c] for c in range(phases)]
            for c in range(phases):
                H[c, b] = h[c]
            for y in range(cy):
                ids = AG[pl.ds((b - 1) * cy + y, 1), :]
                acc = acc + jnp.where(agg_iota == ids, h[0][y : y + 1], 0.0)
        sums = jnp.broadcast_to(jnp.sum(acc, axis=1, keepdims=True), (aggs, tile))
        for g in range(nw):
            y = jnp.sum(CI[:, g * tile : (g + 1) * tile] * sums, axis=0, keepdims=True)
            for k in range(3):
                YB[s, (g + 1 - k) % nw, k : k + 1] = y
        share = [remote(YB.at[s, lax.rem(me_w + d[0], nw)], GB.at[s, k], gs.at[s], gr.at[s], d)
                 for k, d in enumerate(peers)]
        for c in share:
            c.start()
        for b, applied in operate(read, (0, box - 1)):
            for c in range(phases):
                H[c, b] = COEF[first_rhs + c, b + 1] - applied[c]

        for b in range(box):
            out = product(b, scaled(b, [H[c, b] for c in range(phases)]), ring_rows if b in inner else near_rows)
            for c in range(phases):
                W1[c, b + 1] = out[c]

        for b, applied in operate(lambda c, idx: W1[c, idx], range(box)):
            q = scaled(b, [H[c, b] - applied[c] for c in range(phases)])
            out = product(b, q, near_rows if b in inner else None)
            n = 2 * cy if b in inner else cy
            for c in range(phases):
                W2[c, b + 1, :n] = W1[c, b + 1, :n] + out[c]

        for b, applied in operate(lambda c, idx: W2[c, idx], inner):
            out = product(b, scaled(b, [H[c, b] - applied[c] for c in range(phases)]), None)
            for c in range(phases):
                CUR[s + 1, c, b + 1, :cy] = read(c, b + 1)[:cy] + (W2[c, b + 1, :cy] + out[c])

        sent = halo(s + 1)
        start_all([sent[k] for k in UP_FIRST], [sent[k] for k in DOWN_FIRST])
        for c in halo(s):
            c.wait_send()
        pltpu.make_async_copy(GB.at[s], GB.at[s], gs.at[s]).wait()
        pltpu.make_async_copy(GB.at[s], GB.at[s], gr.at[s]).wait()
        total = YB[s, me_w]
        for k in range(len(peers)):
            total = total + GB[s, k]
        tables = [jnp.broadcast_to(total[k : k + 1], (2 * cy, tile)) for k in range(3)]
        for c in halo(s + 1):
            c.wait_recv()
        for p in range(px + 4):
            table = tables[0 if p < 2 else 1 if p < 2 + px else 2]
            lifted = jnp.take_along_axis(table, AGX[p], axis=1, mode="promise_in_bounds")
            FIX[p] = CUR[s + 1, 0, p] + lifted
        return carry

    for c in halo(0):
        c.wait_recv()
    for p in range(px + 4):
        FIX[p] = CUR[0, 0, p]
    for c in aggregates:
        c.wait_recv()
    lax.fori_loop(0, SWEEPS, sweep, 0)
    last = current(SWEEPS)
    for c in range(phases):
        for p in range(px):
            out_it[c, p] = last(c, p + 2)[:cy]
    for b, applied in operate(last, inner):
        for c in range(phases):
            out_res[c, b - 1] = COEF[first_rhs + c, b + 1, 0:cy] - applied[c][:cy]
    for c in halo(SWEEPS) + coef + aggregates:
        c.wait_send()


def solution(mesh):
    nw, nn = mesh.shape["wide"], mesh.shape["narrow"]

    def per_device(rhs, start, trans, accum, coupling, well_cells, well_index, agg_map, tile_factors, coarse_inverse):
        phases, px, cy, tile = rhs.shape
        box = px + 2
        aggs = coarse_inverse.shape[0]
        conn = well_cells.size
        nch = 4 + phases * phases + phases
        vmem = pl.BlockSpec(memory_space=pltpu.VMEM)
        hbm = pl.BlockSpec(memory_space=pl.ANY)
        shape = jax.ShapeDtypeStruct(rhs.shape, F32)
        ring = (2 * cy, tile)
        dma = pltpu.SemaphoreType.DMA
        call = pl.pallas_call(
            functools.partial(body, nw, nn),
            out_shape=(pltpu.VMEM(rhs.shape, F32), pltpu.VMEM(rhs.shape, F32)),
            in_specs=[hbm] * 10,
            out_specs=(vmem, vmem),
            scratch_shapes=[
                pltpu.VMEM((nch, px + 4) + ring, F32),
                pltpu.VMEM((SWEEPS + 1, phases, px + 4) + ring, F32),
                pltpu.VMEM((px + 4,) + ring, F32),
                pltpu.VMEM((phases, px + 4) + ring, F32),
                pltpu.VMEM((phases, px + 4) + ring, F32),
                pltpu.VMEM((phases, box) + ring, F32),
                pltpu.VMEM((4 + 2 * phases, box) + ring, F32),
                pltpu.VMEM(tile_factors.shape, tile_factors.dtype),
                pltpu.VMEM((box, (cy // 2 + 2) * tile, 2 * tile), tile_factors.dtype),
                pltpu.VMEM(coarse_inverse.shape, F32),
                pltpu.VMEM((px * cy, tile), jnp.int32),
                pltpu.VMEM((px + 4,) + ring, jnp.int32),
                pltpu.VMEM(accum.shape, F32),
                pltpu.VMEM((1, conn), jnp.int32),
                pltpu.VMEM((1, conn), F32),
                pltpu.VMEM((SWEEPS, nw * nn - 1, 3, tile), F32),
                pltpu.VMEM((SWEEPS, nw, 3, tile), F32),
                dma((10,)),
                dma((SWEEPS + 1, len(DIRS))),
                dma((SWEEPS + 1, len(DIRS))),
                dma((22,)),
                dma((22,)),
                dma((SWEEPS,)),
                dma((SWEEPS,)),
                dma((len(DIRS),)),
                dma((len(DIRS),)),
                pltpu.SemaphoreType.REGULAR,
                pltpu.SemaphoreType.REGULAR((max(nw, nn),)),
            ],
            compiler_params=pltpu.CompilerParams(collective_id=0, has_side_effects=True),
            name="schwarz",
        )
        held = call(
            rhs, start, trans, accum,
            coupling.reshape((phases * phases,) + accum.shape),
            well_cells.reshape(1, -1), well_index.reshape(1, -1),
            agg_map.reshape(px * cy, tile), tile_factors, coarse_inverse)
        return held

    return jax.shard_map(
        per_device,
        mesh=mesh,
        in_specs=(
            P(None, "wide", "narrow", None),
            P(None, "wide", "narrow", None),
            P(None, "wide", "narrow", None),
            P("wide", "narrow", None),
            P(None, None, "wide", "narrow", None),
            P("wide", "narrow", None),
            P("wide", "narrow", None),
            P("wide", "narrow", None),
            P("wide", "narrow", None, None),
            P(("wide", "narrow"), None),
        ),
        out_specs=(P(None, "wide", "narrow", None), P(None, "wide", "narrow", None)),
        check_vma=False,
    )
```

time: 40.4 us -> 35.1 us (0.87)
  Pallas kernels: 39.5 us -> 33 us
  local copies, waits for them, and re-layouts: 0 us -> 1.24 us
    pallas_call x1, Pallas kernels: 38 us -> 33 us  [per_device(): call(rhs, start, trans, accum, coupling.reshape((phases * phases,) + accu...]
    pallas_call x1 -> x0, Pallas kernels: 1.46 us -> none  [per_device(): pl.pallas_call(hand_over, out_shape=(shape, shape), in_specs=[vmem, vmem]...]
    unnamed x0 -> x2, local copies, waits for them, and re-layouts: none -> 1.24 us
where the time goes in v1:
time: 35.1 us; the launch traced here: 34.9 us
  Pallas kernels  33 us (94%)
  local copies, waits for them, and re-layouts  1.24 us (4%)
  between operations  0.64 us (2%)
    pallas_call x1, Pallas kernels, per_device(): call(rhs, start, trans, accum, coupling.reshape((phases * phases,) + accu...  33 us
    unnamed x2, local copies, waits for them, and re-layouts  1.24 us

profile of v1, /device:TPU:0, one launch (start us, length us, event | category | flops | bytes accessed | tf_op | source)
XLA Modules:
  0.0 34.9 jit_solution(2227162245954185202)
XLA Ops:
  0.6 33.0 %schwarz.1 = (f32[3,4,8,128]{3,2,1,0:T(8,128)S(1)}, f32[3,4,8,128]{3,2,1,0:T(8,128)S(1)}) custom-call(f32[3,4,8,128]{3,2,1,0:T(8,128)} %rhs.1, f32[3,4,8,128]{3,2,1,0:T(8,128)} %start.1, f32[3,4,8,128]{3,2,1,0:T(8,128)} %trans.1, f32[4,8,128]{2,1,0:T(8,128)} %accum.1, f32[9,4,8,128]{3,2,1,0:T(8,128)} %bitcast.4, s32[1,64]{1,0:T(1,128)} %bitcast.6, ...), custom_call_target="tpu_custom_call" | custom-call | tf_op jit(solution)/shard_map/schwarz/pallas_call | solution.py:408
  33.7 0.6 %copy.14 = f32[3,4,8,128]{3,2,1,0:T(8,128)} copy(f32[3,4,8,128]{3,2,1,0:T(8,128)S(1)} %get-tuple-element.2) | data formatting | bytes 98304
  34.3 0.6 %copy.15 = f32[3,4,8,128]{3,2,1,0:T(8,128)} copy(f32[3,4,8,128]{3,2,1,0:T(8,128)S(1)} %get-tuple-element.3) | data formatting | bytes 98304

commit v2 on v1

--- a/solution.py
+++ b/solution.py
@@ -22,6 +22,15 @@
     if t < cy:
         return t + 2
     return t + 2 if t < cy + 2 else t - cy - 2
+
+
+def mirror(me, k, n):
+    out, bit = 0, 1
+    while bit < n:
+        own = lax.rem(me // bit, 2)
+        out = out + bit * (1 - own if (k // bit) % 2 else own)
+        bit *= 2
+    return out
 
 
 def halo_piece(d, px, cy, depth_x, depth_y):
@@ -45,8 +54,8 @@
     nw, nn,
     rhs, start, trans, accum, coupling, cells, widx, agg, tiles, cinv,
     out_it, out_res,
-    COEF, CUR, FIX, W1, W2, H, DER, TF, WT, CI, AG, AGX, ACC, CELLS, WIDX, GB, YB,
-    loc, hs, hr, cs, cr, gs, gr, is_, ir, near, far,
+    COEF, CUR, FIX, W1, W2, H, DER, TF, WT, CI, AG, AGX, ACC, CELLS, WIDX, GB, YB, XT, YT,
+    loc, hs, hr, cs, cr, gs, gr, is_, ir, ts, tr, near, far,
 ):
     phases = rhs.shape[0]
     px, cy, tile = accum.shape
@@ -78,7 +87,9 @@
     for c in local:
         c.start()
 
-    peers = [(dw, dn) for dw in range(nw) for dn in range(nn) if dw or dn]
+    pairs = [(a, c) for a in reversed(range(nw)) for c in reversed(range(nn)) if a or c]
+    mirror_w = [mirror(me_w, a, nw) for a in range(nw)]
+    mirror_n = [mirror(me_n, c, nn) for c in range(nn)]
 
     def signal(sem, d):
         pl.semaphore_signal(sem, inc=1, device_id=dev(*d), device_id_type=pl.DeviceIdType.MESH)
@@ -112,17 +123,24 @@
 
     pieces = []
     for d in DIRS:
-        depth_y = 1 if d[0] < 0 else 2
+        corner = d[0] != 0 and d[1] != 0
+        depth_y = 1 if d[0] else 2
         src, dst = halo_piece(d, px, cy, 1, depth_y)
-        main = [send_coef(pl.ds(1, nch - 1), src, dst, d)]
+        skip = TY if corner and d[0] > 0 else TX
+        main = [send_coef(pl.ds(skip, nch - skip), src, dst, d)]
         rest = [send_coef(pl.ds(ACW, 1), src, dst, d)]
-        if d[0] > 0:
-            (_, sr), (_, dr) = src, dst
-            rest.append(send_coef(pl.ds(1, 1), (pl.ds(px, 1), sr), (pl.ds(0, 1), dr), d))
+        if corner and d[0] > 0:
+            src2, dst2 = halo_piece(d, px, cy, 2, 2)
+            rest.append(send_coef(pl.ds(TX, 1), src2, dst2, d))
+        elif d[0] > 0:
+            rest.append(send_coef(pl.ds(TX, 1), (pl.ds(px, 1), src[1]), (pl.ds(0, 1), dst[1]), d))
         if d[1] > 0:
-            (sp, _), (dp, _) = src, dst
-            rest.append(send_coef(pl.ds(2, 1), (sp, pl.ds(cy - depth_y - 1, 1)), (dp, pl.ds(2 * cy - depth_y - 1, 1)), d))
+            rest.append(send_coef(pl.ds(TY, 1), (src[0], pl.ds(cy - depth_y - 1, 1)), (dst[0], pl.ds(2 * cy - depth_y - 1, 1)), d))
         pieces.append((main, rest))
+    thin = [
+        remote(COEF.at[TX, px + 1, top], XT, ts.at[0], tr.at[0], (1, 0)),
+        remote(COEF.at[TY, own, pl.ds(cy - 1, 1)], YT, ts.at[1], tr.at[1], (0, 1)),
+    ]
     for k in UP_FIRST:
         bulk[0].extend(pieces[k][0])
         late[0].extend(pieces[k][1])
@@ -153,7 +171,10 @@
         signal(near, d)
     begin = halo(0)
     start_all([begin[k] for k in UP_FIRST], [begin[k] for k in DOWN_FIRST])
-    for c in (local[3], local[5], local[6]):
+    local[3].wait()
+    for c in thin:
+        c.start()
+    for c in (local[5], local[6]):
         c.wait()
     start_all(*bulk)
     conn = cells.shape[-1]
@@ -184,6 +205,23 @@
             w[c, box + 1] = zero16
         W2[c, 1] = zero16
         W2[c, box] = zero16
+    rounds, reach = [], 2
+    while reach < max(nw // 2, nn // 2):
+        ws = (0,) if reach >= nw // 2 else (-reach, 0, reach)
+        ns = (0,) if reach >= nn // 2 else (-reach, 0, reach)
+        rounds.append([(a, c) for a in ws for c in ns if a or c])
+        reach *= 2
+
+    def join(opening):
+        for k, group in enumerate(rounds):
+            if opening == (k == 0):
+                for d in group:
+                    signal(far.at[k], d)
+            if not opening:
+                pl.semaphore_wait(far.at[k], len(group))
+
+    pl.semaphore_wait(near, len(DIRS))
+    join(True)
     local[9].wait()
     half_y = cy // 2
     for b in range(box):
@@ -191,19 +229,54 @@
             if t < cy:
                 kb, nb = t % half_y, t // half_y
             else:
-                kb, nb = half_y + (t - cy) % 2, (t - cy) // 2
+                kb, nb = half_y + (t != cy and t != cy + 3), (t - cy) // 2
             WT[b, kb * tile : (kb + 1) * tile, nb * tile : (nb + 1) * tile] = TF[b, slot(t, cy)].T
-    pl.semaphore_wait(near, len(DIRS))
-    reach, k = 2, 0
-    while reach < max(nw // 2, nn // 2):
-        ws = (0,) if reach >= nw // 2 else (-reach, 0, reach)
-        ns = (0,) if reach >= nn // 2 else (-reach, 0, reach)
-        ring_of = [(a, c) for a in ws for c in ns if a or c]
-        for d in ring_of:
-            signal(far.at[k], d)
-        pl.semaphore_wait(far.at[k], len(ring_of))
-        reach, k = 2 * reach, k + 1
+    join(False)
+    agg_iota = lax.broadcasted_iota(jnp.int32, (aggs, tile), 0)
+
+    def gather(acc, p, h):
+        for y in range(cy):
+            ids = AG[pl.ds(p * cy + y, 1), :]
+            acc = acc + jnp.where(agg_iota == ids, h[y : y + 1], 0.0)
+        return acc
+
+    def solve_coarse(s, acc):
+        sums = jnp.broadcast_to(jnp.sum(acc, axis=1, keepdims=True), (aggs, tile))
+        for g in range(nw):
+            y = jnp.sum(CI[:, g * tile : (g + 1) * tile] * sums, axis=0, keepdims=True)
+            for k in range(3):
+                YB[s, (g + 1 - k) % nw, k : k + 1] = y
+        return [
+            pltpu.make_async_remote_copy(
+                src_ref=YB.at[s, mirror_w[a]], dst_ref=GB.at[s, k], send_sem=gs.at[s], recv_sem=gr.at[s],
+                device_id={"wide": mirror_w[a], "narrow": mirror_n[c]}, device_id_type=pl.DeviceIdType.MESH)
+            for k, (a, c) in enumerate(pairs)]
+
     local[8].wait()
+    begin = halo(0)
+    for c in begin + thin:
+        c.wait_recv()
+    acc = jnp.zeros((aggs, tile), F32)
+    for p in range(px):
+        idx = p + 2
+        v, e, w = CUR[0, 0, idx], CUR[0, 0, idx + 1, :cy], CUR[0, 0, idx - 1, :cy]
+        o = v[:cy]
+        lo = low[:cy]
+        tx, ty, tz = (COEF[k, idx, :cy] for k in (TX, TY, TZ))
+        txw = jnp.where(lo, roll(XT[...] if p == 0 else COEF[TX, idx - 1, :cy], half, 1), roll(tx, half, 1))
+        tys = jnp.where(lax.broadcasted_iota(jnp.int32, (cy, tile), 0) == 0, YT[p], roll(ty, 1, 0))
+        tz = jnp.where(lane[:cy] % half < half - 1, tz, 0.0)
+        tzd = roll(tz, 1, 1)
+        turned = roll(o, half, 1)
+        total = (COEF[ACW, idx, :cy] + (tx + txw + ty + tys + tz + tzd) + COEF[4, idx, :cy]) * o
+        for k in range(1, phases):
+            total = total + COEF[4 + k, idx, :cy] * CUR[0, k, idx, :cy]
+        inflow = tx * jnp.where(lo, turned, roll(e, half, 1)) + txw * jnp.where(lo, roll(w, half, 1), turned)
+        inflow = inflow + ty * roll(v, 2 * cy - 1, 0)[:cy] + tys * roll(v, 1, 0)[:cy]
+        inflow = inflow + tz * roll(o, tile - 1, 1) + tzd * roll(o, 1, 1)
+        acc = gather(acc, p, COEF[first_rhs, idx, :cy] - (total - inflow))
+    for c in solve_coarse(0, acc):
+        c.start()
     for c in coef:
         c.wait_recv()
 
@@ -254,8 +327,8 @@
     row = lax.broadcasted_iota(jnp.int32, (2 * cy, tile), 0)
     upper_half = ((row >= half_y) & (row < cy)) | (row >= 2 * cy - 2)
     own_blocks = [(row < cy) & (row % half_y == j) for j in range(half_y)]
-    near_rows = (row == cy, row == 2 * cy - 1)
-    ring_rows = ((row == cy) | (row == 2 * cy - 2), (row == cy + 1) | (row == 2 * cy - 1))
+    near_rows = ((row == cy) | (row == 2 * cy - 1),)
+    ring_rows = near_rows + ((row == cy + 1) | (row == 2 * cy - 2),)
 
     def product(b, q, extra):
         n = cy if extra is None else 2 * cy
@@ -272,85 +345,138 @@
     def scaled(b, h):
         return [DER[4 + phases + c, b] * h[c] for c in range(phases)]
 
-    agg_iota = lax.broadcasted_iota(jnp.int32, (aggs, tile), 0)
-
     def current(e):
         return lambda c, idx: FIX[idx] if c == 0 else CUR[e, c, idx]
 
-    def sweep(s, carry):
-        read = current(s)
-        acc = jnp.zeros((aggs, tile), F32)
-        for b, applied in operate(read, inner):
-            h = [COEF[first_rhs + c, b + 1] - applied[c] for c in range(phases)]
-            for c in range(phases):
-                H[c, b] = h[c]
-            for y in range(cy):
-                ids = AG[pl.ds((b - 1) * cy + y, 1), :]
-                acc = acc + jnp.where(agg_iota == ids, h[0][y : y + 1], 0.0)
-        sums = jnp.broadcast_to(jnp.sum(acc, axis=1, keepdims=True), (aggs, tile))
-        for g in range(nw):
-            y = jnp.sum(CI[:, g * tile : (g + 1) * tile] * sums, axis=0, keepdims=True)
-            for k in range(3):
-                YB[s, (g + 1 - k) % nw, k : k + 1] = y
-        share = [remote(YB.at[s, lax.rem(me_w + d[0], nw)], GB.at[s, k], gs.at[s], gr.at[s], d)
-                 for k, d in enumerate(peers)]
-        for c in share:
-            c.start()
-        for b, applied in operate(read, (0, box - 1)):
-            for c in range(phases):
-                H[c, b] = COEF[first_rhs + c, b + 1] - applied[c]
-
-        for b in range(box):
-            out = product(b, scaled(b, [H[c, b] for c in range(phases)]), ring_rows if b in inner else near_rows)
-            for c in range(phases):
-                W1[c, b + 1] = out[c]
-
-        for b, applied in operate(lambda c, idx: W1[c, idx], range(box)):
-            q = scaled(b, [H[c, b] - applied[c] for c in range(phases)])
-            out = product(b, q, near_rows if b in inner else None)
-            n = 2 * cy if b in inner else cy
-            for c in range(phases):
-                W2[c, b + 1, :n] = W1[c, b + 1, :n] + out[c]
-
-        for b, applied in operate(lambda c, idx: W2[c, idx], inner):
-            out = product(b, scaled(b, [H[c, b] - applied[c] for c in range(phases)]), None)
-            for c in range(phases):
-                CUR[s + 1, c, b + 1, :cy] = read(c, b + 1)[:cy] + (W2[c, b + 1, :cy] + out[c])
-
-        sent = halo(s + 1)
-        start_all([sent[k] for k in UP_FIRST], [sent[k] for k in DOWN_FIRST])
-        for c in halo(s):
+    def drain(e):
+        for c in halo(e):
             c.wait_send()
-        pltpu.make_async_copy(GB.at[s], GB.at[s], gs.at[s]).wait()
-        pltpu.make_async_copy(GB.at[s], GB.at[s], gr.at[s]).wait()
-        total = YB[s, me_w]
-        for k in range(len(peers)):
-            total = total + GB[s, k]
-        tables = [jnp.broadcast_to(total[k : k + 1], (2 * cy, tile)) for k in range(3)]
-        for c in halo(s + 1):
-            c.wait_recv()
-        for p in range(px + 4):
-            table = tables[0 if p < 2 else 1 if p < 2 + px else 2]
-            lifted = jnp.take_along_axis(table, AGX[p], axis=1, mode="promise_in_bounds")
-            FIX[p] = CUR[s + 1, 0, p] + lifted
-        return carry
-
-    for c in halo(0):
-        c.wait_recv()
+
+    def share_done(s, sem):
+        pltpu.make_async_copy(GB.at[s], GB.at[s], sem.at[s]).wait()
+
+    def run(up):
+        order = tuple(range(box)) if up else tuple(reversed(range(box)))
+        close, distant = order[:-2], order[-2:]
+        behind = [k for k, d in enumerate(DIRS) if d[0] == (-1 if up else 1)]
+        ahead = [k for k in range(len(DIRS)) if k not in behind]
+        side = [k for k, d in enumerate(DIRS) if not d[0]]
+        faraway = (px + 2, px + 3) if up else (0, 1)
+
+        def lift(e, tables, slots):
+            for p in slots:
+                table = tables[0 if p < 2 else 1 if p < 2 + px else 2]
+                lifted = jnp.take_along_axis(table, AGX[p], axis=1, mode="promise_in_bounds")
+                FIX[p] = CUR[e, 0, p] + lifted
+
+        def receive(e):
+            share_done(e - 1, gs)
+            landed = halo(e)
+            for k in ahead:
+                landed[k].wait_recv()
+            share_done(e - 1, gr)
+            total = YB[e - 1, me_w]
+            for k in range(len(pairs)):
+                total = total + GB[e - 1, k]
+            tables = [jnp.broadcast_to(total[k : k + 1], (2 * cy, tile)) for k in range(3)]
+            lift(e, tables, [p for p in range(px + 4) if p not in faraway])
+
+            def rest():
+                for k in behind:
+                    landed[k].wait_recv()
+                lift(e, tables, faraway)
+
+            return rest
+
+        def begin_box(read, boxes, acc):
+            for b, applied in operate(read, boxes):
+                h = [COEF[first_rhs + c, b + 1] - applied[c] for c in range(phases)]
+                for c in range(phases):
+                    H[c, b] = h[c]
+                out = product(b, scaled(b, h), ring_rows if b in inner else near_rows)
+                for c in range(phases):
+                    W1[c, b + 1] = out[c]
+                if acc is not None and b in inner:
+                    acc = gather(acc, b - 1, h[0])
+            return acc
+
+        def sweep(s, first):
+            read = current(s)
+            if first:
+                begin_box(read, order, None)
+            else:
+                rest = receive(s)
+                acc = begin_box(read, close, jnp.zeros((aggs, tile), F32))
+                rest()
+                acc = begin_box(read, distant, acc)
+                for c in solve_coarse(s, acc):
+                    c.start()
+            for b, applied in operate(lambda c, idx: W1[c, idx], order):
+                q = scaled(b, [H[c, b] - applied[c] for c in range(phases)])
+                out = product(b, q, near_rows if b in inner else None)
+                n = 2 * cy if b in inner else cy
+                for c in range(phases):
+                    W2[c, b + 1, :n] = W1[c, b + 1, :n] + out[c]
+            done = []
+            for b, applied in operate(lambda c, idx: W2[c, idx], order[1:-1]):
+                done.append((b, product(b, scaled(b, [H[c, b] - applied[c] for c in range(phases)]), None)))
+            sent = halo(s + 1)
+            for part, ks in ((done[:2], behind), (done[2:], [k for k in ahead if k not in side] + side)):
+                for b, out in part:
+                    for c in range(phases):
+                        CUR[s + 1, c, b + 1, :cy] = read(c, b + 1)[:cy] + (W2[c, b + 1, :cy] + out[c])
+                for k in ks:
+                    sent[k].start()
+            drain(s)
+            if first:
+                for c in coef + thin + aggregates:
+                    c.wait_send()
+                for c in aggregates:
+                    c.wait_recv()
+
+        def later(s, carry):
+            sweep(s, False)
+            return carry
+
+        sweep(0, True)
+        lax.fori_loop(1, SWEEPS, later, 0)
+        rest = receive(SWEEPS)
+        last = current(SWEEPS)
+        for c in range(phases):
+            for p in range(px):
+                out_it[c, p] = last(c, p + 2)[:cy]
+
+        def finish(boxes):
+            for b, applied in operate(last, boxes):
+                for c in range(phases):
+                    out_res[c, b - 1] = COEF[first_rhs + c, b + 1, 0:cy] - applied[c][:cy]
+
+        finish(close[1:])
+        rest()
+        finish(distant[:1])
+        drain(SWEEPS)
+
     for p in range(px + 4):
         FIX[p] = CUR[0, 0, p]
-    for c in aggregates:
-        c.wait_recv()
-    lax.fori_loop(0, SWEEPS, sweep, 0)
-    last = current(SWEEPS)
-    for c in range(phases):
-        for p in range(px):
-            out_it[c, p] = last(c, p + 2)[:cy]
-    for b, applied in operate(last, inner):
-        for c in range(phases):
-            out_res[c, b - 1] = COEF[first_rhs + c, b + 1, 0:cy] - applied[c][:cy]
-    for c in halo(SWEEPS) + coef + aggregates:
-        c.wait_send()
+
+    @pl.when(odd == 1)
+    def _():
+        run(True)
+
+    @pl.when(odd == 0)
+    def _():
+        run(False)
+
+
+def hand_over(iterate, residual, out_it, out_res, sem):
+    moves = [
+        pltpu.make_async_copy(iterate, out_it, sem.at[0]),
+        pltpu.make_async_copy(residual, out_res, sem.at[1]),
+    ]
+    for c in moves:
+        c.start()
+    for c in moves:
+        c.wait()
 
 
 def solution(mesh):
@@ -390,6 +516,8 @@
                 pltpu.VMEM((1, conn), F32),
                 pltpu.VMEM((SWEEPS, nw * nn - 1, 3, tile), F32),
                 pltpu.VMEM((SWEEPS, nw, 3, tile), F32),
+                pltpu.VMEM((cy, tile), F32),
+                pltpu.VMEM((px, 1, tile), F32),
                 dma((10,)),
                 dma((SWEEPS + 1, len(DIRS))),
                 dma((SWEEPS + 1, len(DIRS))),
@@ -399,6 +527,8 @@
                 dma((SWEEPS,)),
                 dma((len(DIRS),)),
                 dma((len(DIRS),)),
+                dma((2,)),
+                dma((2,)),
                 pltpu.SemaphoreType.REGULAR,
                 pltpu.SemaphoreType.REGULAR((max(nw, nn),)),
             ],
@@ -410,7 +540,11 @@
             coupling.reshape((phases * phases,) + accum.shape),
             well_cells.reshape(1, -1), well_index.reshape(1, -1),
             agg_map.reshape(px * cy, tile), tile_factors, coarse_inverse)
-        return held
+        held = [pltpu.with_memory_space_constraint(x, pltpu.VMEM) for x in held]
+        return pl.pallas_call(
+            hand_over, out_shape=(shape, shape), in_specs=[vmem, vmem], out_specs=(hbm, hbm),
+            scratch_shapes=[dma((2,))], name="hand_over",
+        )(*held)
 
     return jax.shard_map(
         per_device,

time: 35.1 us -> 33.1 us (0.943)
  local copies, waits for them, and re-layouts: 1.24 us -> 0 us
  Pallas kernels: 33 us -> 32.4 us
    pallas_call x1, Pallas kernels: 33 us -> 31.7 us  [per_device(): call(rhs, start, trans, accum, coupling.reshape((phases * phases,) + accu...]
    unnamed x2 -> x0, local copies, waits for them, and re-layouts: 1.24 us -> none
    pallas_call x0 -> x1, Pallas kernels: none -> 0.66 us  [per_device(): pl.pallas_call(hand_over, out_shape=(shape, shape), in_specs=[vmem, vmem]...]
where the time goes in v2:
time: 33.1 us; the launch traced here: 33 us
  Pallas kernels  32.4 us (98%)
  between operations  0.64 us (2%)
    pallas_call x1, Pallas kernels, per_device(): call(rhs, start, trans, accum, coupling.reshape((phases * phases,) + accu...  31.7 us

profile of v2, /device:TPU:0, one launch (start us, length us, event | category | flops | bytes accessed | tf_op | source)
XLA Modules:
  0.0 33.0 jit_solution(2526141392711840928)
XLA Ops:
  0.6 31.7 %schwarz.1 = (f32[3,4,8,128]{3,2,1,0:T(8,128)S(1)}, f32[3,4,8,128]{3,2,1,0:T(8,128)S(1)}) custom-call(f32[3,4,8,128]{3,2,1,0:T(8,128)} %rhs.1, f32[3,4,8,128]{3,2,1,0:T(8,128)} %start.1, f32[3,4,8,128]{3,2,1,0:T(8,128)} %trans.1, f32[4,8,128]{2,1,0:T(8,128)} %accum.1, f32[9,4,8,128]{3,2,1,0:T(8,128)} %bitcast.4, s32[1,64]{1,0:T(1,128)} %bitcast.6, ...), custom_call_target="tpu_custom_call" | custom-call | tf_op jit(solution)/shard_map/schwarz/pallas_call | solution.py:538
  32.3 0.7 %hand_over.1 = (f32[3,4,8,128]{3,2,1,0:T(8,128)}, f32[3,4,8,128]{3,2,1,0:T(8,128)}) custom-call(f32[3,4,8,128]{3,2,1,0:T(8,128)S(1)} %get-tuple-element.4.iterate, f32[3,4,8,128]{3,2,1,0:T(8,128)S(1)} %get-tuple-element.5.residual), custom_call_target="tpu_custom_call" | custom-call | tf_op jit(solution)/shard_map/hand_over/pallas_call | solution.py:544

commit v3 on v2

--- a/solution.py
+++ b/solution.py
@@ -13,6 +13,7 @@
 F32 = jnp.float32
 
 DIRS = ((-1, 0), (1, 0), (0, -1), (0, 1), (-1, -1), (-1, 1), (1, -1), (1, 1))
+FACES, CORNERS = DIRS[:4], DIRS[4:]
 UP_FIRST = (1, 6, 7, 2, 3, 0, 4, 5)
 DOWN_FIRST = (0, 4, 5, 2, 3, 1, 6, 7)
 ACW, TX, TY, TZ = range(4)
@@ -54,7 +55,7 @@
     nw, nn,
     rhs, start, trans, accum, coupling, cells, widx, agg, tiles, cinv,
     out_it, out_res,
-    COEF, CUR, FIX, W1, W2, H, DER, TF, WT, CI, AG, AGX, ACC, CELLS, WIDX, GB, YB, XT, YT,
+    COEF, CUR, FIX, W1, W2, H, DER, TF, WT, CI, AG, AGX, ACC, CELLS, WIDX, GB, YB, XT, YT, SECOND, PACK, LAND,
     loc, hs, hr, cs, cr, gs, gr, is_, ir, ts, tr, near, far,
 ):
     phases = rhs.shape[0]
@@ -106,13 +107,51 @@
             device_id=dev(*d), device_id_type=pl.DeviceIdType.MESH,
         )
 
+    def copy(src, dst, e, k, d):
+        return remote(src, dst, hs.at[e, k], hr.at[e, k], d)
+
+    def rings(e, depth_y):
+        out = []
+        for k, d in enumerate(FACES):
+            src, dst = halo_piece(d, px, cy, 1, depth_y)
+            out.append(copy(CUR.at[(e, slice(None)) + src], CUR.at[(e, slice(None)) + dst], e, k, d))
+        return out
+
+    def extras(e):
+        n = len(FACES)
+        out = [copy(SECOND.at[e, k], CUR.at[e, pl.ds(0, 2), 0 if d[0] > 0 else px + 3, top], e, n + k, d)
+               for k, d in enumerate(FACES[:2])]
+        return out + [copy(PACK.at[e, k], LAND.at[e, k], e, n + 2 + k, d) for k, d in enumerate(CORNERS)]
+
     def halo(e):
-        out = []
-        for k, d in enumerate(DIRS):
-            src, dst = halo_piece(d, px, cy, 2, 2 if d[0] else 3)
-            out.append(remote(CUR.at[(e, slice(None)) + src], CUR.at[(e, slice(None)) + dst],
-                              hs.at[e, k], hr.at[e, k], d))
-        return out
+        return rings(e, 3) + extras(e)
+
+    def pack(e):
+        lower = lax.broadcasted_iota(jnp.int32, (cy, tile), 1) < half
+        for k, d in enumerate(FACES[:2]):
+            p = px if d[0] > 0 else 3
+            one, two = CUR[e, 1, p, :cy], pltpu.roll(CUR[e, 2, p, :cy], half, 1)
+            SECOND[e, k, 0] = CUR[e, 0, p, :cy]
+            SECOND[e, k, 1] = jnp.where(lower, two, one) if d[0] > 0 else jnp.where(lower, one, two)
+        for k, d in enumerate(CORNERS):
+            p = px + 1 if d[0] > 0 else 2
+            y0, y1 = (cy - 1, cy - 2) if d[1] > 0 else (0, 1)
+            for c in range(phases):
+                PACK[e, k, pl.ds(2 * c, 1)] = CUR[e, c, p, pl.ds(y0, 1)]
+                PACK[e, k, pl.ds(2 * c + 1, 1)] = CUR[e, c, p, pl.ds(y1, 1)]
+            for c in range(2):
+                PACK[e, k, pl.ds(2 * phases + c, 1)] = SECOND[e, 1 if d[0] > 0 else 0, c, pl.ds(y0, 1)]
+
+    def unpack(e, corners):
+        for k in corners:
+            d = CORNERS[k]
+            p, q = (1, 0) if d[0] > 0 else (px + 2, px + 3)
+            y0, y1 = (2 * cy - 1, 2 * cy - 2) if d[1] > 0 else (cy, cy + 1)
+            for c in range(phases):
+                CUR[e, c, p, pl.ds(y0, 1)] = LAND[e, k, pl.ds(2 * c, 1)]
+                CUR[e, c, p, pl.ds(y1, 1)] = LAND[e, k, pl.ds(2 * c + 1, 1)]
+            for c in range(2):
+                CUR[e, c, q, pl.ds(y0, 1)] = LAND[e, k, pl.ds(2 * phases + c, 1)]
 
     coef, bulk, late = [], ([], []), ([], [])
 
@@ -166,11 +205,13 @@
                 c.start()
 
     local[4].wait()
+    pack(0)
     pl.semaphore_wait(barrier, len(DIRS))
     for d in DIRS:
         signal(near, d)
     begin = halo(0)
-    start_all([begin[k] for k in UP_FIRST], [begin[k] for k in DOWN_FIRST])
+    for c in begin:
+        c.start()
     local[3].wait()
     for c in thin:
         c.start()
@@ -256,6 +297,7 @@
     begin = halo(0)
     for c in begin + thin:
         c.wait_recv()
+    unpack(0, range(len(CORNERS)))
     acc = jnp.zeros((aggs, tile), F32)
     for p in range(px):
         idx = p + 2
@@ -277,30 +319,30 @@
         acc = gather(acc, p, COEF[first_rhs, idx, :cy] - (total - inflow))
     for c in solve_coarse(0, acc):
         c.start()
-    for c in coef:
-        c.wait_recv()
-
-    for b in range(box):
-        tx = COEF[TX, b + 1]
-        txw = jnp.where(low, roll(COEF[TX, b], half, 1), roll(tx, half, 1))
-        ty = COEF[TY, b + 1]
-        tys = roll(ty, 1, 0)
-        tz = jnp.where(lane % half < half - 1, COEF[TZ, b + 1], 0.0)
-        tzd = roll(tz, 1, 1)
-        centre = COEF[ACW, b + 1] + (tx + txw + ty + tys + tz + tzd)
-        DER[0, b] = txw
-        DER[1, b] = tys
-        DER[2, b] = tz
-        DER[3, b] = tzd
-        for c in range(phases):
-            diag = centre + COEF[4 + c * phases + c, b + 1]
-            DER[4 + c, b] = diag
-            DER[4 + phases + c, b] = 1.0 / diag
-
-    def operate(read, boxes):
+    def derive(boxes):
+        for b in boxes:
+            tx = COEF[TX, b + 1]
+            txw = jnp.where(low, roll(COEF[TX, b], half, 1), roll(tx, half, 1))
+            ty = COEF[TY, b + 1]
+            tys = roll(ty, 1, 0)
+            tz = jnp.where(lane % half < half - 1, COEF[TZ, b + 1], 0.0)
+            tzd = roll(tz, 1, 1)
+            centre = COEF[ACW, b + 1] + (tx + txw + ty + tys + tz + tzd)
+            DER[0, b] = txw
+            DER[1, b] = tys
+            DER[2, b] = tz
+            DER[3, b] = tzd
+            for c in range(phases):
+                diag = centre + COEF[4 + c * phases + c, b + 1]
+                DER[4 + c, b] = diag
+                DER[4 + phases + c, b] = 1.0 / diag
+
+    def operate(read, boxes, packed=False):
         swapped = {}
 
         def swap(c, idx):
+            if packed and c == 2 and idx in (0, px + 3):
+                return read(1, idx)
             if (c, idx) not in swapped:
                 swapped[c, idx] = roll(read(c, idx), half, 1)
             return swapped[c, idx]
@@ -360,8 +402,21 @@
         close, distant = order[:-2], order[-2:]
         behind = [k for k, d in enumerate(DIRS) if d[0] == (-1 if up else 1)]
         ahead = [k for k in range(len(DIRS)) if k not in behind]
-        side = [k for k, d in enumerate(DIRS) if not d[0]]
         faraway = (px + 2, px + 3) if up else (0, 1)
+
+        def opening(derive, close, distant):
+            for k in ahead:
+                for c in pieces[k][0] + pieces[k][1]:
+                    c.wait_recv()
+            derive(close)
+
+            def rest():
+                for k in behind:
+                    for c in pieces[k][0] + pieces[k][1]:
+                        c.wait_recv()
+                derive(distant)
+
+            return rest
 
         def lift(e, tables, slots):
             for p in slots:
@@ -370,26 +425,35 @@
                 FIX[p] = CUR[e, 0, p] + lifted
 
         def receive(e):
+            final = isinstance(e, int)
             share_done(e - 1, gs)
-            landed = halo(e)
-            for k in ahead:
-                landed[k].wait_recv()
+            landed = rings(e, 1) if final else halo(e)
+            late_faces = [FACES.index((-1 if up else 1, 0))]
+            late_corners = [k for k, d in enumerate(CORNERS) if d[0] == (-1 if up else 1)]
+            slow = late_faces if final else late_faces + [len(FACES) + late_faces[0]] + [len(FACES) + 2 + k for k in late_corners]
+            for k in range(len(landed)):
+                if k not in slow:
+                    landed[k].wait_recv()
             share_done(e - 1, gr)
             total = YB[e - 1, me_w]
             for k in range(len(pairs)):
                 total = total + GB[e - 1, k]
             tables = [jnp.broadcast_to(total[k : k + 1], (2 * cy, tile)) for k in range(3)]
+            if not final:
+                unpack(e, [k for k in range(len(CORNERS)) if k not in late_corners])
             lift(e, tables, [p for p in range(px + 4) if p not in faraway])
 
             def rest():
-                for k in behind:
+                for k in slow:
                     landed[k].wait_recv()
+                if not final:
+                    unpack(e, late_corners)
                 lift(e, tables, faraway)
 
             return rest
 
         def begin_box(read, boxes, acc):
-            for b, applied in operate(read, boxes):
+            for b, applied in operate(read, boxes, True):
                 h = [COEF[first_rhs + c, b + 1] - applied[c] for c in range(phases)]
                 for c in range(phases):
                     H[c, b] = h[c]
@@ -402,31 +466,51 @@
 
         def sweep(s, first):
             read = current(s)
-            if first:
-                begin_box(read, order, None)
-            else:
-                rest = receive(s)
-                acc = begin_box(read, close, jnp.zeros((aggs, tile), F32))
-                rest()
-                acc = begin_box(read, distant, acc)
+            def improve(boxes):
+                for b, applied in operate(lambda c, idx: W1[c, idx], boxes):
+                    q = scaled(b, [H[c, b] - applied[c] for c in range(phases)])
+                    out = product(b, q, near_rows if b in inner else None)
+                    n = 2 * cy if b in inner else cy
+                    for c in range(phases):
+                        W2[c, b + 1, :n] = W1[c, b + 1, :n] + out[c]
+
+            rest = opening(derive, close, distant) if first else receive(s)
+            acc = begin_box(read, close, None if first else jnp.zeros((aggs, tile), F32))
+            improve(order[:0])
+            rest()
+            acc = begin_box(read, distant, acc)
+            if not first:
                 for c in solve_coarse(s, acc):
                     c.start()
-            for b, applied in operate(lambda c, idx: W1[c, idx], order):
-                q = scaled(b, [H[c, b] - applied[c] for c in range(phases)])
-                out = product(b, q, near_rows if b in inner else None)
-                n = 2 * cy if b in inner else cy
-                for c in range(phases):
-                    W2[c, b + 1, :n] = W1[c, b + 1, :n] + out[c]
+            improve(order[0:])
             done = []
             for b, applied in operate(lambda c, idx: W2[c, idx], order[1:-1]):
                 done.append((b, product(b, scaled(b, [H[c, b] - applied[c] for c in range(phases)]), None)))
-            sent = halo(s + 1)
-            for part, ks in ((done[:2], behind), (done[2:], [k for k in ahead if k not in side] + side)):
-                for b, out in part:
-                    for c in range(phases):
-                        CUR[s + 1, c, b + 1, :cy] = read(c, b + 1)[:cy] + (W2[c, b + 1, :cy] + out[c])
-                for k in ks:
-                    sent[k].start()
+            for b, out in done:
+                for c in range(phases):
+                    CUR[s + 1, c, b + 1, :cy] = read(c, b + 1)[:cy] + (W2[c, b + 1, :cy] + out[c])
+            first_face = [1, 0, 2, 3] if up else [0, 1, 2, 3]
+
+            def send_all():
+                ring = rings(s + 1, 3)
+                for k in first_face:
+                    ring[k].start()
+                pack(s + 1)
+                more = extras(s + 1)
+                turn = [1, 4, 5, 0, 2, 3] if up else [0, 2, 3, 1, 4, 5]
+                for k in turn:
+                    more[k].start()
+
+            def send_last():
+                ring = rings(s + 1, 1)
+                for k in first_face:
+                    ring[k].start()
+
+            if first:
+                send_all()
+            else:
+                pl.when(s + 1 < SWEEPS)(send_all)
+                pl.when(s + 1 == SWEEPS)(send_last)
             drain(s)
             if first:
                 for c in coef + thin + aggregates:
@@ -454,7 +538,8 @@
         finish(close[1:])
         rest()
         finish(distant[:1])
-        drain(SWEEPS)
+        for c in rings(SWEEPS, 1):
+            c.wait_send()
 
     for p in range(px + 4):
         FIX[p] = CUR[0, 0, p]
@@ -518,9 +603,12 @@
                 pltpu.VMEM((SWEEPS, nw, 3, tile), F32),
                 pltpu.VMEM((cy, tile), F32),
                 pltpu.VMEM((px, 1, tile), F32),
+                pltpu.VMEM((SWEEPS, 2, 2, cy, tile), F32),
+                pltpu.VMEM((SWEEPS, len(CORNERS), 2 * phases + 2, tile), F32),
+                pltpu.VMEM((SWEEPS, len(CORNERS), 2 * phases + 2, tile), F32),
                 dma((10,)),
-                dma((SWEEPS + 1, len(DIRS))),
-                dma((SWEEPS + 1, len(DIRS))),
+                dma((SWEEPS + 1, len(DIRS) + 2)),
+                dma((SWEEPS + 1, len(DIRS) + 2)),
                 dma((22,)),
                 dma((22,)),
                 dma((SWEEPS,)),

time: 33.1 us -> 32 us (0.967)
  Pallas kernels: 32.4 us -> 31.2 us
    pallas_call x1, Pallas kernels: 31.7 us -> 30.5 us  [per_device(): call(rhs, start, trans, accum, coupling.reshape((phases * phases,) + accu...]
where the time goes in v3:
time: 32 us; the launch traced here: 31.8 us
  Pallas kernels  31.2 us (98%)
  between operations  0.64 us (2%)
    pallas_call x1, Pallas kernels, per_device(): call(rhs, start, trans, accum, coupling.reshape((phases * phases,) + accu...  30.5 us
    pallas_call x1, Pallas kernels, per_device(): pl.pallas_call(hand_over, out_shape=(shape, shape), in_specs=[vmem, vmem]...  0.66 us

profile of v3, /device:TPU:0, one launch (start us, length us, event | category | flops | bytes accessed | tf_op | source)
XLA Modules:
  0.0 31.8 jit_solution(9414105612740677058)
XLA Ops:
  0.6 30.5 %schwarz.1 = (f32[3,4,8,128]{3,2,1,0:T(8,128)S(1)}, f32[3,4,8,128]{3,2,1,0:T(8,128)S(1)}) custom-call(f32[3,4,8,128]{3,2,1,0:T(8,128)} %rhs.1, f32[3,4,8,128]{3,2,1,0:T(8,128)} %start.1, f32[3,4,8,128]{3,2,1,0:T(8,128)} %trans.1, f32[4,8,128]{2,1,0:T(8,128)} %accum.1, f32[9,4,8,128]{3,2,1,0:T(8,128)} %bitcast.4, s32[1,64]{1,0:T(1,128)} %bitcast.6, ...), custom_call_target="tpu_custom_call" | custom-call | tf_op jit(solution)/shard_map/schwarz/pallas_call | solution.py:626
  31.2 0.7 %hand_over.1 = (f32[3,4,8,128]{3,2,1,0:T(8,128)}, f32[3,4,8,128]{3,2,1,0:T(8,128)}) custom-call(f32[3,4,8,128]{3,2,1,0:T(8,128)S(1)} %get-tuple-element.4.iterate, f32[3,4,8,128]{3,2,1,0:T(8,128)S(1)} %get-tuple-element.5.residual), custom_call_target="tpu_custom_call" | custom-call | tf_op jit(solution)/shard_map/hand_over/pallas_call | solution.py:632

commit v4 on v3

--- a/solution.py
+++ b/solution.py
@@ -16,7 +16,7 @@
 FACES, CORNERS = DIRS[:4], DIRS[4:]
 UP_FIRST = (1, 6, 7, 2, 3, 0, 4, 5)
 DOWN_FIRST = (0, 4, 5, 2, 3, 1, 6, 7)
-ACW, TX, TY, TZ = range(4)
+TX, ACW, TY, TZ = range(4)
 
 
 def slot(t, cy):
@@ -76,13 +76,14 @@
         (cells, CELLS),
         (widx, WIDX),
         (accum, ACC),
-        (trans, COEF.at[pl.ds(1, 3), own, top]),
+        (trans.at[pl.ds(0, 1)], COEF.at[pl.ds(TX, 1), own, top]),
         (start, CUR.at[0, :, own, top]),
         (coupling, COEF.at[pl.ds(4, phases * phases), own, top]),
         (rhs, COEF.at[pl.ds(first_rhs, phases), own, top]),
         (agg, AG),
         (cinv, CI),
         (tiles, TF),
+        (trans.at[pl.ds(1, 2)], COEF.at[pl.ds(TY, 2), own, top]),
     ]
     local = [pltpu.make_async_copy(s, d, loc.at[k]) for k, (s, d) in enumerate(copies)]
     for c in local:
@@ -165,9 +166,9 @@
         corner = d[0] != 0 and d[1] != 0
         depth_y = 1 if d[0] else 2
         src, dst = halo_piece(d, px, cy, 1, depth_y)
-        skip = TY if corner and d[0] > 0 else TX
+        skip = ACW if corner and d[0] > 0 else TX
         main = [send_coef(pl.ds(skip, nch - skip), src, dst, d)]
-        rest = [send_coef(pl.ds(ACW, 1), src, dst, d)]
+        rest = []
         if corner and d[0] > 0:
             src2, dst2 = halo_piece(d, px, cy, 2, 2)
             rest.append(send_coef(pl.ds(TX, 1), src2, dst2, d))
@@ -213,11 +214,11 @@
     for c in begin:
         c.start()
     local[3].wait()
+    local[10].wait()
     for c in thin:
         c.start()
     for c in (local[5], local[6]):
         c.wait()
-    start_all(*bulk)
     conn = cells.shape[-1]
     for c in local[:3]:
         c.wait()
@@ -229,6 +230,7 @@
     right = jnp.where(hit_l, 1.0, 0.0)
     wells = lax.dot_general(left, right, NT, precision=HIGHEST, preferred_element_type=F32)
     COEF[ACW, 2 : 2 + px, 0:cy, :] = ACC[...] + wells.reshape(px, cy, tile)
+    start_all(*bulk)
     start_all(*late)
     local[7].wait()
     AGX[2 : 2 + px, 0:cy] = (AG[...] + me_n * aggs).reshape(px, cy, tile)
@@ -418,10 +420,15 @@
 
             return rest
 
-        def lift(e, tables, slots):
+        def lifts(tables, slots):
+            out = []
             for p in slots:
                 table = tables[0 if p < 2 else 1 if p < 2 + px else 2]
-                lifted = jnp.take_along_axis(table, AGX[p], axis=1, mode="promise_in_bounds")
+                out.append((p, jnp.take_along_axis(table, AGX[p], axis=1, mode="promise_in_bounds")))
+            return out
+
+        def lift(e, found):
+            for p, lifted in found:
                 FIX[p] = CUR[e, 0, p] + lifted
 
         def receive(e):
@@ -435,20 +442,22 @@
                 if k not in slow:
                     landed[k].wait_recv()
             share_done(e - 1, gr)
-            total = YB[e - 1, me_w]
-            for k in range(len(pairs)):
-                total = total + GB[e - 1, k]
+            parts = [YB[e - 1, me_w]] + [GB[e - 1, k] for k in range(len(pairs))]
+            while len(parts) > 1:
+                parts = [sum(parts[k : k + 2][1:], parts[k]) for k in range(0, len(parts), 2)]
+            total = parts[0]
             tables = [jnp.broadcast_to(total[k : k + 1], (2 * cy, tile)) for k in range(3)]
             if not final:
                 unpack(e, [k for k in range(len(CORNERS)) if k not in late_corners])
-            lift(e, tables, [p for p in range(px + 4) if p not in faraway])
+            lift(e, lifts(tables, [p for p in range(px + 4) if p not in faraway]))
+            ready = lifts(tables, faraway)
 
             def rest():
                 for k in slow:
                     landed[k].wait_recv()
                 if not final:
                     unpack(e, late_corners)
-                lift(e, tables, faraway)
+                lift(e, ready)
 
             return rest
 
@@ -606,11 +615,11 @@
                 pltpu.VMEM((SWEEPS, 2, 2, cy, tile), F32),
                 pltpu.VMEM((SWEEPS, len(CORNERS), 2 * phases + 2, tile), F32),
                 pltpu.VMEM((SWEEPS, len(CORNERS), 2 * phases + 2, tile), F32),
-                dma((10,)),
+                dma((11,)),
                 dma((SWEEPS + 1, len(DIRS) + 2)),
                 dma((SWEEPS + 1, len(DIRS) + 2)),
-                dma((22,)),
-                dma((22,)),
+                dma((14,)),
+                dma((14,)),
                 dma((SWEEPS,)),
                 dma((SWEEPS,)),
                 dma((len(DIRS),)),

time: 32 us -> 31.7 us (level)
    pallas_call x1, Pallas kernels: 30.5 us -> 30.2 us  [per_device(): call(rhs, start, trans, accum, coupling.reshape((phases * phases,) + accu...]
where the time goes in v4:
time: 31.7 us; the launch traced here: 31.5 us
  Pallas kernels  30.9 us (97%)
  between operations  0.64 us (2%)
    pallas_call x1, Pallas kernels, per_device(): call(rhs, start, trans, accum, coupling.reshape((phases * phases,) + accu...  30.2 us
    pallas_call x1, Pallas kernels, per_device(): pl.pallas_call(hand_over, out_shape=(shape, shape), in_specs=[vmem, vmem]...  0.66 us

profile of v4, /device:TPU:0, one launch (start us, length us, event | category | flops | bytes accessed | tf_op | source)
XLA Modules:
  0.0 31.5 jit_solution(5810049066181059531)
XLA Ops:
  0.6 30.2 %schwarz.1 = (f32[3,4,8,128]{3,2,1,0:T(8,128)S(1)}, f32[3,4,8,128]{3,2,1,0:T(8,128)S(1)}) custom-call(f32[3,4,8,128]{3,2,1,0:T(8,128)} %rhs.1, f32[3,4,8,128]{3,2,1,0:T(8,128)} %start.1, f32[3,4,8,128]{3,2,1,0:T(8,128)} %trans.1, f32[4,8,128]{2,1,0:T(8,128)} %accum.1, f32[9,4,8,128]{3,2,1,0:T(8,128)} %bitcast.4, s32[1,64]{1,0:T(1,128)} %bitcast.6, ...), custom_call_target="tpu_custom_call" | custom-call | tf_op jit(solution)/shard_map/schwarz/pallas_call | solution.py:635
  30.8 0.7 %hand_over.1 = (f32[3,4,8,128]{3,2,1,0:T(8,128)}, f32[3,4,8,128]{3,2,1,0:T(8,128)}) custom-call(f32[3,4,8,128]{3,2,1,0:T(8,128)S(1)} %get-tuple-element.4.iterate, f32[3,4,8,128]{3,2,1,0:T(8,128)S(1)} %get-tuple-element.5.residual), custom_call_target="tpu_custom_call" | custom-call | tf_op jit(solution)/shard_map/hand_over/pallas_call | solution.py:641

commit v5 on v4

--- a/solution.py
+++ b/solution.py
@@ -206,12 +206,14 @@
                 c.start()
 
     local[4].wait()
-    pack(0)
     pl.semaphore_wait(barrier, len(DIRS))
     for d in DIRS:
         signal(near, d)
     begin = halo(0)
-    for c in begin:
+    for c in begin[:4]:
+        c.start()
+    pack(0)
+    for c in begin[4:]:
         c.start()
     local[3].wait()
     local[10].wait()

time: 31.7 us -> 31.7 us (level)
  no operation moved by 1% of the time
where the time goes in v5:
time: 31.7 us; the launch traced here: 31.5 us
  Pallas kernels  30.9 us (97%)
  between operations  0.64 us (2%)
    pallas_call x1, Pallas kernels, per_device(): call(rhs, start, trans, accum, coupling.reshape((phases * phases,) + accu...  30.2 us
    pallas_call x1, Pallas kernels, per_device(): pl.pallas_call(hand_over, out_shape=(shape, shape), in_specs=[vmem, vmem]...  0.66 us

profile of v5, /device:TPU:0, one launch (start us, length us, event | category | flops | bytes accessed | tf_op | source)
XLA Modules:
  0.0 31.5 jit_solution(12672652117158137921)
XLA Ops:
  0.6 30.2 %schwarz.1 = (f32[3,4,8,128]{3,2,1,0:T(8,128)S(1)}, f32[3,4,8,128]{3,2,1,0:T(8,128)S(1)}) custom-call(f32[3,4,8,128]{3,2,1,0:T(8,128)} %rhs.1, f32[3,4,8,128]{3,2,1,0:T(8,128)} %start.1, f32[3,4,8,128]{3,2,1,0:T(8,128)} %trans.1, f32[4,8,128]{2,1,0:T(8,128)} %accum.1, f32[9,4,8,128]{3,2,1,0:T(8,128)} %bitcast.4, s32[1,64]{1,0:T(1,128)} %bitcast.6, ...), custom_call_target="tpu_custom_call" | custom-call | tf_op jit(solution)/shard_map/schwarz/pallas_call | solution.py:637
  30.9 0.7 %hand_over.1 = (f32[3,4,8,128]{3,2,1,0:T(8,128)}, f32[3,4,8,128]{3,2,1,0:T(8,128)}) custom-call(f32[3,4,8,128]{3,2,1,0:T(8,128)S(1)} %get-tuple-element.4.iterate, f32[3,4,8,128]{3,2,1,0:T(8,128)S(1)} %get-tuple-element.5.residual), custom_call_target="tpu_custom_call" | custom-call | tf_op jit(solution)/shard_map/hand_over/pallas_call | solution.py:643
